TPU v7x, 768 devices: a whole 4x8x12 slice. The times are simulated.
768 devices in a mesh: sub: 96 (over z_lo, y, core), in: 8 (over x, z_hi).
Axes of the slice: x: 4, y: 8, z: 12 (z_hi: 2, z_lo: 6; z = z_hi * 6 + z_lo), core: 2. Of those that a mesh axis runs over, the one named last changes fastest.
Arguments:
- body_load: float32 [4, 64, 32, 12288], P(None, 'in', None, 'sub'), may hold values from -6 to 6
- materials: int32 [64, 32, 12288], P('in', None, 'sub'), may hold values from 0 to 7
- material_tables: float32 [8, 4, 4], replicated
- corner_index: int32 [6144], P(('sub', 'in')), may hold values from 0 to 1023
- coarse_inverse: float32 [6144, 6144], P(('sub', 'in')), as said below
Outputs:
- interior_solution: float32 [4, 64, 32, 12288], P(None, 'in', None, 'sub')
- interface_sum: float32 [96, 4, 64, 32], P('sub', None, 'in')
Inputs may be any that keep to these rules, and one draw needn't show every extreme that they name: coarse_inverse is symmetric.
All inputs are finite; a program needn't handle non-finite values.
Results may differ from a plain program's by a relative error of at most 0.0003.
Values sent between devices are 32-bit elements; how exact they have to be, the bound alone decides.
A program may use at most 32 MiB of HBM per device.

v0:
```python
import jax
import jax.numpy as jnp
from jax import lax
from jax.sharding import PartitionSpec as P

NMAT = 8
ITERS = 3


def copy_for_each(x, axis):
    length = lax.axis_size(axis)
    return lax.all_to_all(jnp.broadcast_to(x[None], (length, *x.shape)), axis, 0, 0, tiled=True)


def over_copies(x, axis):
    everything = copy_for_each(x, axis)
    return jnp.sum(everything, axis=0)


def packed_total(arrays, axis):
    ravelled, at, done = (jnp.concatenate([a.reshape(-1) for a in arrays]), 0, [])
    subtotal = over_copies(ravelled, axis)
    for a in arrays:
        done.append(subtotal[at : at + a.size].reshape(a.shape))
        at += a.size
    return tuple(done)


def extended_2(cells, sides, width):
    for axis, dim in sides:
        count = lax.axis_size(axis)
        ends = count - 1
        head = lax.slice_in_dim(cells, 0, width, axis=dim)
        tail = lax.slice_in_dim(cells, cells.shape[dim] - width, cells.shape[dim], axis=dim)
        cells = jnp.concatenate(
            [
                lax.ppermute(tail, axis, [(i, (i + 1) % count) for i in range(ends)]),
                cells,
                lax.ppermute(head, axis, [((i + 1) % count, i) for i in range(ends)]),
            ],
            axis=dim,
        )
    return cells


def passed_along(x, axis, by):
    length = lax.axis_size(axis)
    return lax.ppermute(x, axis, [(i, (i + by) % length) for i in range(length)])


def node_tables(material, tables):
    total = jnp.zeros((tables.shape[1], tables.shape[2]) + material.shape, jnp.float32)
    for material_kind in range(NMAT):
        chosen = (material == material_kind).astype(jnp.float32)
        total = total + chosen[None, None] * tables[material_kind][:, :, None, None, None]
    return total


def stencil(padded, center, gains):
    padded = jnp.pad(padded, ((0, 0), (0, 0), (1, 1), (1, 1)))
    beside = padded[:, 2:, 1:-1, 1:-1] + padded[:, :-2, 1:-1, 1:-1]
    beside = beside + padded[:, 1:-1, 2:, 1:-1] + padded[:, 1:-1, :-2, 1:-1]
    beside = beside + padded[:, 1:-1, 1:-1, 2:] + padded[:, 1:-1, 1:-1, :-2]
    coupled = jnp.sum(gains * center[None], axis=1)
    return 6.0 * center + coupled - beside


def fit_layers(values, like_layers):
    cut = (values.shape[1] - like_layers) // 2
    return values[:, cut : cut + like_layers]


def two_products(residual, applied):
    return packed_total((jnp.sum(residual * residual), jnp.sum(residual * applied)), "in")


def on_device(body_load, materials, material_tables, corner_index, coarse_inverse):
    layers = body_load.shape[1]
    stacked = jnp.concatenate([body_load, materials.astype(jnp.float32)[None]], axis=0)
    extended = extended_2(stacked, (("in", 1),), ITERS)
    start_load = extended[:-1]
    gains_all = node_tables(extended[-1].astype(jnp.int32), material_tables)
    layer_ids = (
        lax.axis_index("in") * layers - ITERS + jnp.arange(layers + 2 * ITERS, dtype=jnp.int32)
    )
    inside_all = ((layer_ids >= 0) & (layer_ids < layers * lax.axis_size("in"))).astype(
        jnp.float32
    )[None, :, None, None]

    def apply_operator(values):
        depth = values.shape[1] - 2
        gains = gains_all[
            :, :, (gains_all.shape[2] - depth) // 2 : (gains_all.shape[2] - depth) // 2 + depth
        ]
        inside = fit_layers(inside_all, depth)
        return stencil(values, values[:, 1:-1], gains) * inside

    def own(values):
        return fit_layers(values, layers)

    solution = jnp.zeros_like(start_load)
    residual = start_load
    applied = apply_operator(residual)
    residual = fit_layers(residual, applied.shape[1])
    norm_now, product = two_products(own(residual), own(applied))
    step_size = norm_now / product
    direction, applied_dir = (residual, applied)
    for repeat in range(ITERS):
        solution = fit_layers(solution, direction.shape[1]) + step_size * direction
        residual = residual - step_size * applied_dir
        if repeat + 1 < ITERS:
            applied = apply_operator(residual)
            depth = applied.shape[1]
            residual = fit_layers(residual, depth)
            direction = fit_layers(direction, depth)
            applied_dir = fit_layers(applied_dir, depth)
            solution = fit_layers(solution, depth)
            norm_next, product = two_products(own(residual), own(applied))
            beta_ratio = norm_next / norm_now
            step_size = norm_next / (product - beta_ratio * norm_next / step_size)
            direction = residual + beta_ratio * direction
            applied_dir = applied + beta_ratio * applied_dir
            norm_now = norm_next
    solution = own(solution)
    residual = own(residual)
    right_face = residual[..., -1]
    left_face = residual[..., 0]
    from_next = passed_along(left_face, "sub", -1)
    summed = (right_face + from_next).reshape(-1)
    coarse_local = jnp.take(summed, corner_index)
    gathered = lax.all_gather(coarse_local, ("sub", "in"), axis=0, tiled=True)
    coarse_solution = jnp.dot(coarse_inverse, gathered, precision=lax.Precision.HIGHEST)
    corrected = summed.at[corner_index].add(coarse_solution)
    interface_sum = corrected.reshape((1,) + right_face.shape)
    return (solution, interface_sum)


def solution(mesh):
    return jax.shard_map(
        on_device,
        mesh=mesh,
        in_specs=(
            P(None, "in", None, "sub"),
            P("in", None, "sub"),
            P(),
            P(("sub", "in")),
            P(("sub", "in"), None),
        ),
        out_specs=(P(None, "in", None, "sub"), P("sub", None, "in", None)),
        check_vma=False,
    )
```

profile of v0, /device:TPU:1, one launch (start us, length us, event | category | flops | bytes accessed | tf_op | source)
XLA Modules:
  0.0 258.5 jit_solution(1375821625770706531)
XLA Ops:
  0.6 0.0 copy-start
  0.6 1.0 convert_bitcast_fusion.8
  1.6 1.1 pad_maximum_fusion.2
  2.7 15.7 %collective-permute-start = (f32[5,3,32,128]{3,2,1,0:T(8,128)S(1)}, f32[5,3,32,128]{3,2,1,0:T(8,128)S(1)}, u32[]{:S(2)}, u32[]{:S(2)}) collective-permute-start(f32[5,3,32,128]{3,2,1,0:T(8,128)S(1)} %get-tuple-element.39), channel_id=1, source_target_pairs={{0,1},{1,2},{2,3},{3,4},{4,5},{5,6},{6,7},{8,9},{9,10},{10,11},{11... | collective-permute-start | bytes 737288 | tf_op jit(solution)/shard_map/ppermute | solution.py:37
  18.4 1.3 collective-permute-start.1
  19.7 1.2 slice_reduce_fusion.9
  20.9 0.1 slice_bitcast_fusion.2
  21.0 2.1 collective-permute-done
  23.0 19.9 %collective-permute-done.1 = f32[5,3,32,128]{3,2,1,0:T(8,128)S(1)} collective-permute-done((f32[5,3,32,128]{3,2,1,0:T(8,128)S(1)}, f32[5,3,32,128]{3,2,1,0:T(8,128)S(1)}, u32[]{:S(2)}, u32[]{:S(2)}) %collective-permute-start.1) | collective-permute-done | bytes 245792 | tf_op jit(solution)/shard_map/ppermute | solution.py:39
  43.0 1.1 pad_maximum_fusion
  44.1 0.2 convert_bitcast_fusion.7
  44.3 0.1 slice.243
  44.4 0.1 slice.248
  44.4 2.3 multiply_add_fusion
  46.8 0.0 copy-start.1
  46.8 1.8 copy-done.1
  48.6 0.5 fusion
  49.1 0.7 fusion.8
  49.8 0.0 copy-start.4
  49.8 0.9 copy-done.4
  50.6 0.0 copy-done.5
  50.7 0.8 multiply_reduce_fusion.3
  51.4 1.4 pad_maximum_fusion.3
  52.8 0.6 broadcast_in_dim.12
  53.4 5.8 %all-to-all-start = ((f32[8,1,2]{2,1,0:T(1,128)}), f32[8,1,2]{2,1,0:T(1,128)S(1)}, u32[]{:S(2)}, u32[]{:S(2)}) async-start(f32[8,1,2]{2,1,0:T(1,128)} %broadcast_in_dim.12), calls=%async_computation | async-start | bytes 8192 | tf_op jit(solution)/shard_map/all_to_all | solution.py:12
  59.2 0.1 slice_bitcast_fusion.1
  59.3 11.2 %all-to-all-done = f32[8,1,2]{2,1,0:T(1,128)S(1)} async-done(((f32[8,1,2]{2,1,0:T(1,128)}), f32[8,1,2]{2,1,0:T(1,128)S(1)}, u32[]{:S(2)}, u32[]{:S(2)}) %all-to-all-start) | async-done | bytes 96 | tf_op jit(solution)/shard_map/all_to_all | solution.py:12
  70.5 0.6 fusion.35
  72.3 0.0 copy-start.2
  72.3 1.5 multiply_subtract_fusion
  73.9 0.7 copy-done.2
  74.6 0.4 fusion.1
  75.0 0.4 fusion.14
  75.5 0.9 multiply_reduce_fusion.2
  76.3 1.4 pad_maximum_fusion.4
  77.7 0.6 broadcast_in_dim.13
  78.3 3.3 %all-to-all-start.1 = ((f32[8,1,2]{2,1,0:T(1,128)}), f32[8,1,2]{2,1,0:T(1,128)S(1)}, u32[]{:S(2)}, u32[]{:S(2)}) async-start(f32[8,1,2]{2,1,0:T(1,128)} %broadcast_in_dim.13), calls=%async_computation.1 | async-start | bytes 8192 | tf_op jit(solution)/shard_map/all_to_all | solution.py:12
  81.7 0.1 slice_bitcast_fusion
  81.7 11.1 %all-to-all-done.1 = f32[8,1,2]{2,1,0:T(1,128)S(1)} async-done(((f32[8,1,2]{2,1,0:T(1,128)}), f32[8,1,2]{2,1,0:T(1,128)S(1)}, u32[]{:S(2)}, u32[]{:S(2)}) %all-to-all-start.1) | async-done | bytes 96 | tf_op jit(solution)/shard_map/all_to_all | solution.py:12
  92.9 0.6 fusion.34
  97.6 0.0 copy-start.3
  97.7 2.6 %multiply_subtract_fusion.1 = (f32[4,10,32,128]{3,2,1,0:T(8,128)S(1)}, f32[4,10,32,128]{3,2,1,0:T(8,128)}, f32[4,10,32,128]{3,2,1,0:T(8,128)}, f32[4,10,32,128]{3,2,1,0:T(8,128)}) fusion(f32[]{:T(128)S(6)} %div.24, f32[4,12,32,128]{3,2,1,0:T(8,128)S(1)} %multiply_subtract_fusion, f32[4,10,32,128]{3,2,1,0:T(8,128)S(1)} %fusion.14, ...), kind=kLoop, calls=%fused_computation.42 | loop fusion | flops 983040 | bytes 5242888 | tf_op jit(solution)/shard_map/sub | solution.py:110
  100.3 0.0 copy-done.3
  100.3 0.3 fusion.2
  100.7 1.9 multiply_reduce_fusion.1
  102.6 1.4 pad_maximum_fusion.5
  104.0 0.6 broadcast_in_dim.14
  104.6 3.3 %all-to-all-start.2 = ((f32[8,1,2]{2,1,0:T(1,128)}), f32[8,1,2]{2,1,0:T(1,128)S(1)}, u32[]{:S(2)}, u32[]{:S(2)}) async-start(f32[8,1,2]{2,1,0:T(1,128)} %broadcast_in_dim.14), calls=%async_computation.2 | async-start | bytes 8192 | tf_op jit(solution)/shard_map/all_to_all | solution.py:12
  107.9 0.0 copy-done.9
  107.9 11.2 %all-to-all-done.2 = f32[8,1,2]{2,1,0:T(1,128)S(1)} async-done(((f32[8,1,2]{2,1,0:T(1,128)}), f32[8,1,2]{2,1,0:T(1,128)S(1)}, u32[]{:S(2)}, u32[]{:S(2)}) %all-to-all-start.2) | async-done | bytes 96 | tf_op jit(solution)/shard_map/all_to_all | solution.py:12
  119.1 0.6 fusion.33
  123.6 0.0 copy-done.6
  123.6 2.2 fusion.25
  125.8 0.5 slice_reduce_fusion
  126.3 7.4 %collective-permute-start.2 = (f32[4,8,32]{2,1,0:T(8,128)S(1)}, f32[4,8,32]{2,1,0:T(8,128)S(1)}, u32[]{:S(2)}, u32[]{:S(2)}) collective-permute-start(f32[4,8,32]{2,1,0:T(8,128)S(1)} %get-tuple-element.10), channel_id=1, source_target_pairs={{0,760},{8,0},{16,8},{24,16},{32,24},{40,32},{48,40},{56,48},{64,5... | collective-permute-start | bytes 12296 | tf_op jit(solution)/shard_map/ppermute | solution.py:48
  133.7 2.6 collective-permute-done.2
  136.2 0.1 reshape.186
  136.3 0.6 gather_fusion
  137.0 0.1 fusion.30
  137.1 119.5 %all-reduce.3 = f32[6144]{0:T(1024)S(1)} all-reduce(f32[6144]{0:T(1024)S(1)} %fusion.30), channel_id=1, replica_groups=mesh['sub'=96,'in'=8] {'sub','in'}, use_global_device_ids=true, to_apply=%add.3 | all-reduce | flops 6144 | bytes 49152
  256.6 0.0 copy-done
  256.6 0.5 convolution_bitcast_fusion
  257.2 0.6 scatter_fusion
  257.8 0.7 reshape.187
  (17 shorter events, 0.2 us)
Async XLA Ops:
  0.6 256.0 %copy-start = (f32[8,6144]{1,0:T(8,128)S(1)}, f32[8,6144]{1,0:T(8,128)}, u32[]{:S(2)}) copy-start(f32[8,6144]{1,0:T(8,128)} %param.9) | copy-start | bytes 589828
  2.7 20.3 %collective-permute-start = (f32[5,3,32,128]{3,2,1,0:T(8,128)S(1)}, f32[5,3,32,128]{3,2,1,0:T(8,128)S(1)}, u32[]{:S(2)}, u32[]{:S(2)}) collective-permute-start(f32[5,3,32,128]{3,2,1,0:T(8,128)S(1)} %get-tuple-element.39), channel_id=1, source_target_pairs={{0,1},{1,2},{2,3},{3,4},{4,5},{5,6},{6,7},{8,9},{9,10},{10,11},{11... | collective-permute-start | bytes 737288 | tf_op jit(solution)/shard_map/ppermute | solution.py:37
  18.4 24.6 %collective-permute-start.1 = (f32[5,3,32,128]{3,2,1,0:T(8,128)S(1)}, f32[5,3,32,128]{3,2,1,0:T(8,128)S(1)}, u32[]{:S(2)}, u32[]{:S(2)}) collective-permute-start(f32[5,3,32,128]{3,2,1,0:T(8,128)S(1)} %get-tuple-element.40), channel_id=1, source_target_pairs={{1,0},{2,1},{3,2},{4,3},{5,4},{6,5},{7,6},{9,8},{10,9},{11,10},{12... | collective-permute-start | bytes 737288 | tf_op jit(solution)/shard_map/ppermute | solution.py:39
  46.8 1.8 copy-start.1
  48.6 2.1 copy-start.5
  49.8 0.9 copy-start.4
  53.4 17.0 %all-to-all-start = ((f32[8,1,2]{2,1,0:T(1,128)}), f32[8,1,2]{2,1,0:T(1,128)S(1)}, u32[]{:S(2)}, u32[]{:S(2)}) async-start(f32[8,1,2]{2,1,0:T(1,128)} %broadcast_in_dim.12), calls=%async_computation | async-start | bytes 8192 | tf_op jit(solution)/shard_map/all_to_all | solution.py:12
  72.3 2.3 copy-start.2
  78.3 14.5 %all-to-all-start.1 = ((f32[8,1,2]{2,1,0:T(1,128)}), f32[8,1,2]{2,1,0:T(1,128)S(1)}, u32[]{:S(2)}, u32[]{:S(2)}) async-start(f32[8,1,2]{2,1,0:T(1,128)} %broadcast_in_dim.13), calls=%async_computation.1 | async-start | bytes 8192 | tf_op jit(solution)/shard_map/all_to_all | solution.py:12
  97.6 2.7 %copy-start.3 = (f32[4,4,14,32,128]{4,3,2,1,0:T(8,128)S(1)}, f32[4,4,14,32,128]{4,3,2,1,0:T(8,128)}, u32[]{:S(2)}) copy-start(f32[4,4,14,32,128]{4,3,2,1,0:T(8,128)} %copy-done.1) | copy-start | bytes 11010052
  100.3 7.6 %copy-start.9 = (s32[8]{0:T(128)S(1)}, s32[8]{0:T(128)}, u32[]{:S(2)}) copy-start(s32[8]{0:T(128)} %param.8) | copy-start | bytes 100
  100.3 23.3 %copy-start.6 = (f32[4,10,32,128]{3,2,1,0:T(8,128)S(1)}, f32[4,10,32,128]{3,2,1,0:T(8,128)}, u32[]{:S(2)}) copy-start(f32[4,10,32,128]{3,2,1,0:T(8,128)} %get-tuple-element.24) | copy-start | bytes 1966084
  100.3 23.3 %copy-start.7 = (f32[4,10,32,128]{3,2,1,0:T(8,128)S(1)}, f32[4,10,32,128]{3,2,1,0:T(8,128)}, u32[]{:S(2)}) copy-start(f32[4,10,32,128]{3,2,1,0:T(8,128)} %get-tuple-element.35) | copy-start | bytes 1966084
  100.3 23.3 %copy-start.8 = (f32[4,10,32,128]{3,2,1,0:T(8,128)S(1)}, f32[4,10,32,128]{3,2,1,0:T(8,128)}, u32[]{:S(2)}) copy-start(f32[4,10,32,128]{3,2,1,0:T(8,128)} %get-tuple-element.36) | copy-start | bytes 1966084
  104.6 14.5 %all-to-all-start.2 = ((f32[8,1,2]{2,1,0:T(1,128)}), f32[8,1,2]{2,1,0:T(1,128)S(1)}, u32[]{:S(2)}, u32[]{:S(2)}) async-start(f32[8,1,2]{2,1,0:T(1,128)} %broadcast_in_dim.14), calls=%async_computation.2 | async-start | bytes 8192 | tf_op jit(solution)/shard_map/all_to_all | solution.py:12
  126.3 9.9 %collective-permute-start.2 = (f32[4,8,32]{2,1,0:T(8,128)S(1)}, f32[4,8,32]{2,1,0:T(8,128)S(1)}, u32[]{:S(2)}, u32[]{:S(2)}) collective-permute-start(f32[4,8,32]{2,1,0:T(8,128)S(1)} %get-tuple-element.10), channel_id=1, source_target_pairs={{0,760},{8,0},{16,8},{24,16},{32,24},{40,32},{48,40},{56,48},{64,5... | collective-permute-start | bytes 12296 | tf_op jit(solution)/shard_map/ppermute | solution.py:48
where the time goes:
time: 259 us; the launch traced here: 258 us
  blocking collectives  120 us (46%)
  waiting for transfers between devices  58 us (22%)
  starting transfers between devices  36.7 us (14%)
  other arithmetic  22.8 us (9%)
  local copies, waits for them, and re-layouts  10.5 us (4%)
  between operations  10.3 us (4%)
    unnamed x1, blocking collectives  120 us
    all_to_all x3, waiting for transfers between devices, copy_for_each(): lax.all_to_all(jnp.broadcast_to(x[None], (length, *x.shape)), axis, 0, 0,...  33.5 us
    ppermute x1, waiting for transfers between devices, extended_2(): lax.ppermute(head, axis, [((i + 1) % count, i) for i in range(ends)])  19.9 us
    ppermute x1, starting transfers between devices, extended_2(): lax.ppermute(tail, axis, [(i, (i + 1) % count) for i in range(ends)])  15.7 us
    all_to_all x3, starting transfers between devices, copy_for_each(): lax.all_to_all(jnp.broadcast_to(x[None], (length, *x.shape)), axis, 0, 0,...  12.4 us
    ppermute x1, starting transfers between devices, passed_along(): lax.ppermute(x, axis, [(i, (i + by) % length) for i in range(length)])  7.35 us
    sub x3, other arithmetic, on_device(): residual = residual - step_size * applied_dir  6.23 us
  transfers between devices with their start and end apart: 6, of which 6 were waited for; matrix products, arithmetic and copies ran while one was open for 1% of the time, Pallas kernels for 0%

commit v1 on v0

v1 whole, which is shorter than its diff:
```python
import jax
import jax.numpy as jnp
from jax import lax
from jax.experimental import pallas as pl
from jax.experimental.pallas import tpu as pltpu
from jax.sharding import PartitionSpec as P

MESH = pl.DeviceIdType.MESH
COMP, NMAT, ITERS = 4, 8, 3
CZ, PY, PX, KC = 8, 32, 128, 8
N_SUB, N_IN = 96, 8
H = ITERS
EXT = CZ + 2 * H
NY, NZL = 8, 6
CHIPS = N_SUB // 2
PAIRS = [(0, 0), (0, 1), (0, 2), (0, 3), (1, 1), (1, 2), (1, 3), (2, 2), (2, 3)]
ZSTEPS = (1, 2, 3, 10, 11)


def remote(src, dst, send, recv, device):
    return pltpu.make_async_remote_copy(
        src_ref=src, dst_ref=dst, send_sem=send, recv_sem=recv, device_id=device, device_id_type=MESH
    )


def kernel(
    b_hbm, m_hbm, tab, ci_hbm, cinv_hbm,
    sol_hbm, face_hbm,
    v0, v1, v2, v3, mat, gains, cinv, sol, rows, send_row, ex, ag, left_out, left_in, face,
    ci_vec, ci_left_vec, ci_own, ci_left, local_sem, send_sem, recv_sem,
):
    sub, inn = lax.axis_index("sub"), lax.axis_index("in")
    core, y, zl = sub % 2, (sub // 2) % NY, sub // (2 * NY)
    x, z = inn // 2, (inn % 2) * NZL + zl

    def device(core_, y_, z_):
        return {"sub": ((z_ % NZL) * NY + y_) * 2 + core_, "in": x * 2 + z_ // NZL}

    def in_peer(k):
        return {"sub": sub, "in": (inn + k) % N_IN}

    def z_peer(d, other):
        return device((core + other) % 2, y, (z + d) % (2 * NZL))

    def y_peer(k):
        return device(core, (y + k) % NY, z)

    sub_next = {"sub": (sub + 1) % N_SUB, "in": inn}
    sub_prev = {"sub": (sub + N_SUB - 1) % N_SUB, "in": inn}

    load_b = pltpu.make_async_copy(b_hbm, v0.at[:, pl.ds(H, CZ)], local_sem.at[0])
    load_m = pltpu.make_async_copy(m_hbm, mat.at[pl.ds(H, CZ)], local_sem.at[1])
    load_c = pltpu.make_async_copy(ci_hbm, ci_vec, local_sem.at[2])
    load_inv = pltpu.make_async_copy(cinv_hbm, cinv, local_sem.at[3])
    load_own = pltpu.make_async_copy(ci_hbm, ci_own, local_sem.at[4])
    load_b.start()
    load_m.start()
    load_c.start()
    load_own.start()
    load_inv.start()

    barrier = pltpu.get_barrier_semaphore()
    greet = [in_peer(k) for k in range(1, N_IN)]
    greet += [z_peer(d, o) for d in (0, 1, 2, 3, 9, 10, 11) for o in (0, 1) if d or o]
    greet += [y_peer(k) for k in range(1, NY)]
    greet += [sub_next, sub_prev]
    for peer in greet:
        pl.semaphore_signal(barrier, inc=1, device_id=peer, device_id_type=MESH)

    low, high = None, None
    for k in range(NMAT):
        for c in range(COMP):
            centre = tab[k, c, c]
            radius = jnp.float32(6.0)
            for d in range(COMP):
                if d != c:
                    radius = radius + jnp.maximum(tab[k, c, d], -tab[k, c, d])
            lo, hi = centre - radius, centre + radius
            low = lo if low is None else jnp.minimum(low, lo)
            high = hi if high is None else jnp.maximum(high, hi)
    sigma = 6.0 + 0.5 * (low + high)
    width = 0.5 * (high - low)
    inv_row = 1.0 / jnp.full((1, PX), width, jnp.float32)
    shift = 6.0 - sigma

    load_b.wait()
    load_m.wait()
    load_c.wait()
    load_own.wait()
    pl.semaphore_wait(barrier, len(greet))

    up, down = in_peer(1), in_peer(N_IN - 1)
    halos = [
        remote(v0.at[:, pl.ds(CZ, H)], v0.at[:, pl.ds(0, H)], send_sem.at[0], recv_sem.at[0], up),
        remote(v0.at[:, pl.ds(H, H)], v0.at[:, pl.ds(H + CZ, H)], send_sem.at[1], recv_sem.at[1], down),
        remote(mat.at[pl.ds(CZ + 1, 2)], mat.at[pl.ds(1, 2)], send_sem.at[2], recv_sem.at[2], up),
        remote(mat.at[pl.ds(H, 2)], mat.at[pl.ds(H + CZ, 2)], send_sem.at[3], recv_sem.at[3], down),
        remote(ci_vec, ci_left_vec, send_sem.at[4], recv_sem.at[4], sub_next),
    ]
    for copy in halos:
        copy.start()

    lane = lax.broadcasted_iota(jnp.int32, (PY, PX), 1)
    row = lax.broadcasted_iota(jnp.int32, (PY, PX), 0)

    def tables_of(layer):
        ids = mat[layer]
        top, mid, bottom = ids >= 4, (ids & 2) != 0, (ids & 1) != 0
        for c in range(COMP):
            for d in range(COMP):
                pairs = [jnp.where(bottom, tab[2 * k + 1, c, d], tab[2 * k, c, d]) for k in range(4)]
                value = jnp.where(top, jnp.where(mid, pairs[3], pairs[2]), jnp.where(mid, pairs[1], pairs[0]))
                gains[c * COMP + d, layer] = value + shift if c == d else value

    def apply_at(src, layer, scale):
        centre = [src[c, layer] for c in range(COMP)]
        result = []
        for c in range(COMP):
            v = centre[c]
            beside = src[c, layer - 1] + src[c, layer + 1]
            beside = beside + jnp.where(row == 0, 0.0, pltpu.roll(v, 1, 0))
            beside = beside + jnp.where(row == PY - 1, 0.0, pltpu.roll(v, PY - 1, 0))
            beside = beside + jnp.where(lane == 0, 0.0, pltpu.roll(v, 1, 1))
            beside = beside + jnp.where(lane == PX - 1, 0.0, pltpu.roll(v, PX - 1, 1))
            coupled = gains[c * COMP, layer] * centre[0]
            for d in range(1, COMP):
                coupled = coupled + gains[c * COMP + d, layer] * centre[d]
            result.append((coupled - beside) * scale)
        return centre, result

    def layers(lo, hi, body):
        @pl.loop(lo, hi)
        def _(layer):
            body(layer)

    def scale_at(layer):
        at = inn * CZ - H + layer
        keep = jnp.where((at >= 0) & (at < N_IN * CZ), jnp.float32(1.0), jnp.float32(0.0))
        return inv_row * keep

    def advance(src, dst):
        def body(layer):
            _, result = apply_at(src, layer, scale_at(layer))
            for c in range(COMP):
                dst[c, layer] = result[c]

        return body

    first, second = advance(v0, v1), advance(v1, v2)

    def third(layer, sums):
        a2, a3 = apply_at(v2, layer, inv_row)
        a0 = [v0[c, layer] for c in range(COMP)]
        a1 = [v1[c, layer] for c in range(COMP)]
        basis = (a0, a1, a2, a3)
        for c in range(COMP):
            v3[c, layer - H] = a3[c]
        out = []
        for (i, j), total in zip(PAIRS, sums):
            part = basis[i][0] * basis[j][0]
            for c in range(1, COMP):
                part = part + basis[i][c] * basis[j][c]
            out.append(total + ((part[0:8] + part[8:16]) + (part[16:24] + part[24:32])))
        return tuple(out)

    layers(H, H + CZ, tables_of)
    layers(H + 1, H + CZ - 1, first)
    layers(H + 2, H + CZ - 2, second)
    sums = tuple(jnp.zeros((8, PX), jnp.float32) for _ in PAIRS)
    sums = lax.fori_loop(H + 3, H + CZ - 3, third, sums)

    for copy in halos:
        copy.wait()
    load_left = pltpu.make_async_copy(ci_left_vec, ci_left, local_sem.at[5])
    load_left.start()

    @pl.when(inn == 0)
    def _():
        for c in range(COMP):
            v0[c, H - 1] = jnp.zeros((PY, PX), jnp.float32)

    @pl.when(inn == N_IN - 1)
    def _():
        for c in range(COMP):
            v0[c, H + CZ] = jnp.zeros((PY, PX), jnp.float32)

    layers(1, H, tables_of)
    layers(H + CZ, EXT - 1, tables_of)
    layers(1, H + 1, first)
    layers(H + CZ - 1, EXT - 1, first)
    layers(2, H + 2, second)
    layers(H + CZ - 2, EXT - 2, second)
    sums = lax.fori_loop(H, H + 3, third, sums)
    sums = lax.fori_loop(H + CZ - 3, H + CZ, third, sums)
    load_left.wait()

    for j in range(KC):
        for side, ids in ((0, ci_own), (1, ci_left)):
            spot = ids[0, j]
            c, layer, at = spot // (CZ * PY), (spot // PY) % CZ, spot % PY
            place = side * KC + j
            rows[pl.ds(place, 1), :] = v0[c, layer + H, pl.ds(at, 1), :]
            rows[pl.ds(16 + place, 1), :] = v1[c, layer + H, pl.ds(at, 1), :]
            rows[pl.ds(32 + place, 1), :] = v2[c, layer + H, pl.ds(at, 1), :]
            rows[pl.ds(48 + place, 1), :] = v3[c, layer, pl.ds(at, 1), :]
    rows[pl.ds(64, 64), :] = jnp.zeros((64, PX), jnp.float32)
    turned = jnp.transpose(rows[...])
    lane1 = lax.broadcasted_iota(jnp.int32, (1, PX), 1)
    own_row = jnp.where((lane1 // KC) % 2 == 0, turned[PX - 1 : PX, :], turned[0:1, :])
    own_row = jnp.where(lane1 < 64, own_row, 0.0)
    for n, total in enumerate(sums):
        whole = jnp.sum(jnp.sum(total, axis=0, keepdims=True), axis=1, keepdims=True)
        own_row = jnp.where(lane1 == 64 + n, whole, own_row)
    send_row[...] = own_row
    ex[pl.ds(inn, 1), :] = own_row
    gram_copies = []
    for k in range(1, N_IN):
        copy = remote(send_row, ex.at[pl.ds(inn, 1)], send_sem.at[4 + k], recv_sem.at[4 + k], in_peer(k))
        copy.start()
        gram_copies.append(copy)
    for copy in gram_copies:
        copy.wait()

    everyone = ex[...]
    total = jnp.sum(everyone, axis=0, keepdims=True)
    gram = {}
    for n, (i, j) in enumerate(PAIRS):
        value = jnp.sum(jnp.where(lane1 == 64 + n, total, 0.0), axis=1, keepdims=True)
        gram[i, j] = gram[j, i] = value

    def form(p, q, offset):
        value = None
        for i, a in enumerate(p):
            for j, b in enumerate(q):
                term = a * b * gram[i, j + offset]
                value = term if value is None else value + term
        return value

    res = [jnp.ones((1, 1), jnp.float32)]
    direction, previous = list(res), []
    rr = form(res, res, 0)
    dd, beta = rr, None
    answer = [jnp.zeros((1, 1), jnp.float32) for _ in range(ITERS)]
    for step in range(ITERS):
        delta = width * form(direction, direction, 1)
        if step:
            delta = delta + sigma * (beta * beta * dd_before)
        inverse = 1.0 / (sigma * rr + delta)
        alpha = rr * inverse
        for j, value in enumerate(direction):
            answer[j] = answer[j] + alpha * value
        moved = []
        for j in range(step + 2):
            value = None
            if j <= step:
                value = res[j] * delta
                if j < len(previous):
                    value = value - sigma * rr * (beta * previous[j])
                value = value * inverse
            if j:
                part = (alpha * width) * direction[j - 1]
                value = -part if value is None else value - part
            moved.append(value)
        if step + 1 < ITERS:
            new = form(moved, moved, 0)
            beta = new / rr
            previous = direction
            direction = [
                value + beta * direction[j] if j <= step else value for j, value in enumerate(moved)
            ]
            dd_before = dd
            dd = new + beta * beta * dd
            rr = new
        res = moved

    factors = jnp.zeros((1, PX), jnp.float32)
    for k in range(ITERS + 1):
        factors = jnp.where(lane1 // 16 == k, res[k], factors)
    mixed = everyone * factors
    mixed = (mixed + pltpu.roll(mixed, PX - 16, 1)) + (pltpu.roll(mixed, PX - 32, 1) + pltpu.roll(mixed, PX - 48, 1))
    unit = jnp.zeros((1, PX), jnp.float32)
    for i in range(N_IN):
        piece = mixed[i : i + 1, :]
        piece = jnp.where(lane1 < 8, piece, 0.0) + pltpu.roll(jnp.where((lane1 >= 8) & (lane1 < 16), piece, 0.0), 56, 1)
        unit = unit + (pltpu.roll(piece, KC * i, 1) if i else piece)

    def slot(core_):
        return ag.at[pl.ds(y * 16 + zl * 2 + core_, 1)]

    ag[pl.ds(y * 16 + zl * 2 + core, 1), :] = unit
    z_copies = []
    for n, (d, o) in enumerate([(d, o) for d in (0,) + ZSTEPS for o in (0, 1) if d or o]):
        copy = remote(slot(core), slot(core), send_sem.at[12 + n], recv_sem.at[12 + n], z_peer(d, o))
        copy.start()
        z_copies.append(copy)

    wide = [jnp.broadcast_to(value, (1, PX)) for value in res]
    wide_x = [jnp.broadcast_to(value, (1, PX)) for value in answer]

    def finish(layer, faces):
        for c in range(COMP):
            a0, a1, a2, a3 = v0[c, layer + H], v1[c, layer + H], v2[c, layer + H], v3[c, layer]
            sol[c, layer] = wide_x[0] * a0 + wide_x[1] * a1 + wide_x[2] * a2
            left = (wide[0] * a0 + wide[1] * a1) + (wide[2] * a2 + wide[3] * a3)
            place = c * CZ + layer
            faces = jnp.where(lane == place, pltpu.roll(left, place + 1, 1), faces)
            faces = jnp.where(lane == place + 32, pltpu.roll(left, place + 32, 1), faces)
        return faces

    faces = lax.fori_loop(0, CZ, finish, jnp.zeros((PY, PX), jnp.float32))
    store_sol = pltpu.make_async_copy(sol, sol_hbm, local_sem.at[6])
    store_sol.start()
    faces = jnp.transpose(jnp.concatenate([faces, jnp.zeros((PX - PY, PX), jnp.float32)], axis=0))
    left_out[...] = faces[32:64, :]
    left_copy = remote(left_out, left_in, send_sem.at[30], recv_sem.at[30], sub_prev)
    left_copy.start()

    for copy in z_copies:
        copy.wait()
    y_copies = []
    mine = ag.at[pl.ds(y * 16, 12)]
    for k in range(1, NY):
        copy = remote(mine, mine, send_sem.at[22 + k], recv_sem.at[22 + k], y_peer(k))
        copy.start()
        y_copies.append(copy)
    load_inv.wait()
    left_copy.wait()
    summed = faces[0:32, :] + left_in[...]
    for copy in y_copies:
        copy.wait()

    lane8 = lax.broadcasted_iota(jnp.int32, (8, PX), 1)
    row8 = lax.broadcasted_iota(jnp.int32, (8, PX), 0)
    even = [ag[pl.ds(k * 2, NY, stride=16), :] for k in range(NZL)]
    odd = [ag[pl.ds(k * 2 + 1, NY, stride=16), :] for k in range(NZL)]
    turned_even = [pltpu.roll(value, NY - 1, 0) for value in even]
    acc = jnp.zeros((KC, PX), jnp.float32)
    for k in range(NZL):
        after = jnp.where(row8 == NY - 1, turned_even[(k + 1) % NZL], turned_even[k])
        block = jnp.where(lane8 < 64, even[k], after) + pltpu.roll(odd[k], 64, 1)
        for at in range(NY):
            column = (k * NY + at) * PX
            acc = acc + cinv[:, column : column + PX] * block[at : at + 1, :]
    coarse = jnp.sum(acc, axis=1, keepdims=True)
    spots = row * PY + lane
    for j in range(KC):
        hit = (spots == ci_own[0, j]) & (lane < PY)
        summed = summed + jnp.where(hit, coarse[j : j + 1, :], 0.0)
    for c in range(COMP):
        face[0, c] = summed[c * CZ : (c + 1) * CZ, 0:PY]
    store_face = pltpu.make_async_copy(face, face_hbm, local_sem.at[7])
    store_face.start()
    store_sol.wait()
    store_face.wait()


def on_device(body_load, materials, material_tables, corner_index, coarse_inverse):
    f32, i32 = jnp.float32, jnp.int32
    anywhere = pl.BlockSpec(memory_space=pl.ANY)
    return pl.pallas_call(
        kernel,
        out_shape=(
            jax.ShapeDtypeStruct((COMP, CZ, PY, PX), f32),
            jax.ShapeDtypeStruct((1, COMP, CZ, PY), f32),
        ),
        in_specs=[anywhere, anywhere, pl.BlockSpec(memory_space=pltpu.SMEM), anywhere, anywhere],
        out_specs=(anywhere, anywhere),
        scratch_shapes=[
            pltpu.VMEM((COMP, EXT, PY, PX), f32),
            pltpu.VMEM((COMP, EXT, PY, PX), f32),
            pltpu.VMEM((COMP, EXT, PY, PX), f32),
            pltpu.VMEM((COMP, CZ, PY, PX), f32),
            pltpu.VMEM((EXT, PY, PX), i32),
            pltpu.VMEM((COMP * COMP, EXT, PY, PX), f32),
            pltpu.VMEM((KC, N_SUB * N_IN * KC), f32),
            pltpu.VMEM((COMP, CZ, PY, PX), f32),
            pltpu.VMEM((PX, PX), f32),
            pltpu.VMEM((1, PX), f32),
            pltpu.VMEM((N_IN, PX), f32),
            pltpu.VMEM((NY * 16, PX), f32),
            pltpu.VMEM((PY, PX), f32),
            pltpu.VMEM((PY, PX), f32),
            pltpu.VMEM((1, COMP, CZ, PY), f32),
            pltpu.VMEM((1, KC), i32),
            pltpu.VMEM((1, KC), i32),
            pltpu.SMEM((1, KC), i32),
            pltpu.SMEM((1, KC), i32),
            pltpu.SemaphoreType.DMA((8,)),
            pltpu.SemaphoreType.DMA((31,)),
            pltpu.SemaphoreType.DMA((31,)),
        ],
        compiler_params=pltpu.CompilerParams(collective_id=0, has_side_effects=True),
    )(body_load, materials, material_tables, corner_index.reshape(1, KC), coarse_inverse)


def solution(mesh):
    return jax.shard_map(
        on_device,
        mesh=mesh,
        in_specs=(
            P(None, "in", None, "sub"),
            P("in", None, "sub"),
            P(),
            P(("sub", "in")),
            P(("sub", "in"), None),
        ),
        out_specs=(P(None, "in", None, "sub"), P("sub", None, "in", None)),
        check_vma=False,
    )
```

time: 259 us -> 79.4 us (0.31)
  blocking collectives: 120 us -> 0 us
  Pallas kernels: 0 us -> 74.6 us
  waiting for transfers between devices: 58 us -> 0 us
  starting transfers between devices: 36.7 us -> 0 us
  other arithmetic: 22.8 us -> 0 us
  between operations: 10.3 us -> 0.65 us
  local copies, waits for them, and re-layouts: 10.5 us -> 3.88 us
    unnamed x1 -> x0, blocking collectives: 120 us -> none
    pallas_call x0 -> x1, Pallas kernels: none -> 74.6 us  [on_device(): pl.pallas_call(kernel, out_shape=(jax.ShapeDtypeStruct((COMP, CZ, PY, PX)...]
    all_to_all x3 -> x0, waiting for transfers between devices: 33.5 us -> none  [copy_for_each(): lax.all_to_all(jnp.broadcast_to(x[None], (length, *x.shape)), axis, 0, 0,...]
    ppermute x3 -> x0, waiting for transfers between devices: 24.6 us -> none  [the longest x1 19.9 us: extended_2(): lax.ppermute(head, axis, [((i + 1) % count, i) for i in range(ends)])]
    ppermute x3 -> x0, starting transfers between devices: 24.3 us -> none  [the longest x1 15.7 us: extended_2(): lax.ppermute(tail, axis, [(i, (i + 1) % count) for i in range(ends)])]
    all_to_all x3 -> x0, starting transfers between devices: 12.4 us -> none  [copy_for_each(): lax.all_to_all(jnp.broadcast_to(x[None], (length, *x.shape)), axis, 0, 0,...]
    sub x3 -> x0, other arithmetic: 6.23 us -> none  [on_device(): residual = residual - step_size * applied_dir]
    concatenate x4 -> x0, other arithmetic: 5.32 us -> none  [the longest x3 4.18 us: packed_total(): jnp.concatenate([a.reshape(-1) for a in arrays])]
  transfers between devices with their start and end apart: 6 -> 0, of which waited for: 6 -> 0; matrix products, arithmetic and copies ran while one was open for 1% -> 0% of each run, Pallas kernels for 0% -> 0%
where the time goes in v1:
time: 79.4 us; the launch traced here: 79.1 us
  Pallas kernels  74.6 us (94%)
  local copies, waits for them, and re-layouts  3.88 us (5%)
    pallas_call x1, Pallas kernels, on_device(): pl.pallas_call(kernel, out_shape=(jax.ShapeDtypeStruct((COMP, CZ, PY, PX)...  74.6 us
    unnamed x5, local copies, waits for them, and re-layouts  3.88 us

profile of v1, /device:TPU:1, one launch (start us, length us, event | category | flops | bytes accessed | tf_op | source)
XLA Modules:
  0.0 79.1 jit_solution(9711523616451594064)
XLA Ops:
  0.6 1.4 %copy.7.tab = f32[8,4,4]{2,1,0:T(4,128)} copy(f32[8,4,4]{0,2,1:T(4,128)} %param.7) | data formatting | bytes 1024 | tf_op args[2]
  2.0 74.6 %shard_map.68 = (f32[4,8,32,128]{3,2,1,0:T(8,128)}, f32[1,4,8,32]{3,2,1,0:T(8,128)}) custom-call(f32[4,8,32,128]{3,2,1,0:T(8,128)} %b_hbm.1, s32[8,32,128]{2,1,0:T(8,128)} %m_hbm.1, f32[8,4,4]{2,1,0:T(4,128)} %copy.7.tab, s32[1,8]{1,0:T(1,128)} %bitcast.1, f32[8,6144]{1,0:T(8,128)} %cinv_hbm.1), custom_call_target="tpu_custom_call" | custom-call | tf_op jit(solution)/shard_map/pallas_call | solution.py:360
  76.6 0.0 copy-start
  76.6 1.9 %copy.10 = f32[4,8,32,128]{3,2,1,0:T(8,128)} copy(f32[4,8,32,128]{3,2,1,0:T(8,128)} %get-tuple-element.4) | data formatting | bytes 1048576
  78.5 0.0 copy-done
  78.5 0.6 copy.11
Async XLA Ops:
  76.6 1.9 %copy-start = (f32[1,4,8,32]{3,2,1,0:T(8,128)S(1)}, f32[1,4,8,32]{3,2,1,0:T(8,128)}, u32[]{:S(2)}) copy-start(f32[1,4,8,32]{3,2,1,0:T(8,128)} %get-tuple-element.5) | copy-start | bytes 12292

commit v2 on v1

v2 whole, which is shorter than its diff:
```python
import jax
import jax.numpy as jnp
from jax import lax
from jax.experimental import pallas as pl
from jax.experimental.pallas import tpu as pltpu
from jax.sharding import PartitionSpec as P

MESH = pl.DeviceIdType.MESH
COMP, NMAT, ITERS = 4, 8, 3
CZ, PY, PX, KC = 8, 32, 128, 8
N_SUB, N_IN = 96, 8
H = 1
EXT = CZ + 2 * H
FIRST, LAST, BELOW, ABOVE = H, H + CZ - 1, 0, H + CZ
NY, NZL = 8, 6
PAIRS = [(0, 0), (0, 1), (0, 2), (0, 3), (1, 1), (1, 2), (1, 3), (2, 2), (2, 3)]
ZSTEPS = (1, 2, 3, 10, 11)


def remote(src, dst, send, recv, device):
    return pltpu.make_async_remote_copy(
        src_ref=src, dst_ref=dst, send_sem=send, recv_sem=recv, device_id=device, device_id_type=MESH
    )


def kernel(
    b_hbm, m_hbm, tab_hbm, ci_hbm, cinv_hbm,
    sol_out, face_out,
    v0, v1, v2, v3, mat, gains, w1_low, w1_high, w2_low, pack_out, pack_in,
    cinv, rows, send_row, ex, ag, left_out, left_in,
    ci_vec, ci_left_vec, ci_own, ci_left, tab, local_sem, send_sem, recv_sem,
):
    sub, inn = lax.axis_index("sub"), lax.axis_index("in")
    core, y, zl = sub % 2, (sub // 2) % NY, sub // (2 * NY)
    x, z = inn // 2, (inn % 2) * NZL + zl

    def device(core_, y_, z_):
        return {"sub": ((z_ % NZL) * NY + y_) * 2 + core_, "in": x * 2 + z_ // NZL}

    def in_peer(k):
        return {"sub": sub, "in": (inn + k) % N_IN}

    def z_peer(d, other):
        return device((core + other) % 2, y, (z + d) % (2 * NZL))

    def y_peer(k):
        return device(core, (y + k) % NY, z)

    sub_next = {"sub": (sub + 1) % N_SUB, "in": inn}
    sub_prev = {"sub": (sub + N_SUB - 1) % N_SUB, "in": inn}

    barrier = pltpu.get_barrier_semaphore()
    greet = [in_peer(k) for k in (1, N_IN - 1)]
    greet += [in_peer(k) for k in range(2, N_IN - 1)]
    greet += [z_peer(d, o) for d in (0, 1, 2, 3, 9, 10, 11) for o in (0, 1) if d or o]
    greet += [y_peer(k) for k in range(1, NY)]
    greet += [sub_next, sub_prev]
    for peer in greet:
        pl.semaphore_signal(barrier, inc=1, device_id=peer, device_id_type=MESH)

    load_b = pltpu.make_async_copy(b_hbm, v0.at[:, pl.ds(H, CZ)], local_sem.at[0])
    load_m = pltpu.make_async_copy(m_hbm, mat.at[pl.ds(H, CZ)], local_sem.at[1])
    load_t = pltpu.make_async_copy(tab_hbm, tab, local_sem.at[6])
    load_c = pltpu.make_async_copy(ci_hbm, ci_vec, local_sem.at[2])
    load_inv = pltpu.make_async_copy(cinv_hbm, cinv, local_sem.at[3])
    load_own = pltpu.make_async_copy(ci_hbm, ci_own, local_sem.at[4])
    for load in (load_b, load_m, load_t, load_c, load_own, load_inv):
        load.start()
    load_t.wait()

    low, high = None, None
    for k in range(NMAT):
        for c in range(COMP):
            centre = tab[c, c, k]
            radius = jnp.float32(6.0)
            for d in range(COMP):
                if d != c:
                    radius = radius + jnp.maximum(tab[c, d, k], -tab[c, d, k])
            lo, hi = centre - radius, centre + radius
            low = lo if low is None else jnp.minimum(low, lo)
            high = hi if high is None else jnp.maximum(high, hi)
    sigma = 6.0 + 0.5 * (low + high)
    width = 0.5 * (high - low)
    inv_row = 1.0 / jnp.full((1, PX), width, jnp.float32)
    shift = 6.0 - sigma
    keep_low = jnp.where(inn > 0, jnp.float32(1.0), jnp.float32(0.0))
    keep_high = jnp.where(inn < N_IN - 1, jnp.float32(1.0), jnp.float32(0.0))
    cross = -inv_row
    cross_low, cross_high = cross * keep_low, cross * keep_high

    load_b.wait()
    load_m.wait()
    load_c.wait()
    load_own.wait()
    pl.semaphore_wait(barrier, len(greet))

    up, down = in_peer(1), in_peer(N_IN - 1)
    send_b_up = remote(v0.at[:, LAST], v0.at[:, BELOW], send_sem.at[0], recv_sem.at[0], up)
    send_b_down = remote(v0.at[:, FIRST], v0.at[:, ABOVE], send_sem.at[1], recv_sem.at[1], down)
    send_m_down = remote(mat.at[FIRST], mat.at[ABOVE], send_sem.at[2], recv_sem.at[2], down)
    send_w1_up = remote(w1_high, v1.at[:, BELOW], send_sem.at[3], recv_sem.at[3], up)
    send_w1_down = remote(w1_low, v1.at[:, ABOVE], send_sem.at[4], recv_sem.at[4], down)
    send_w2_down = remote(w2_low, v2.at[:, ABOVE], send_sem.at[5], recv_sem.at[5], down)
    send_pack_up = remote(pack_out, pack_in, send_sem.at[6], recv_sem.at[6], up)
    send_ci = remote(ci_vec, ci_left_vec, send_sem.at[7], recv_sem.at[7], sub_next)
    halos = (send_b_up, send_b_down, send_m_down, send_w1_up, send_w1_down, send_w2_down, send_pack_up, send_ci)
    for copy in (send_b_down, send_b_up, send_m_down, send_ci):
        copy.start()

    lane = lax.broadcasted_iota(jnp.int32, (PY, PX), 1)
    row = lax.broadcasted_iota(jnp.int32, (PY, PX), 0)

    def tables_of(layer, ids=None):
        ids = mat[layer] if ids is None else ids
        top, mid, bottom = ids >= 4, (ids & 2) != 0, (ids & 1) != 0
        for c in range(COMP):
            for d in range(COMP):
                pairs = [jnp.where(bottom, tab[c, d, 2 * k + 1], tab[c, d, 2 * k]) for k in range(4)]
                value = jnp.where(top, jnp.where(mid, pairs[3], pairs[2]), jnp.where(mid, pairs[1], pairs[0]))
                gains[c * COMP + d, layer] = value + shift if c == d else value

    def within(centre, layer):
        result = []
        for c in range(COMP):
            v = centre[c]
            beside = jnp.where(row == 0, 0.0, pltpu.roll(v, 1, 0))
            beside = beside + jnp.where(row == PY - 1, 0.0, pltpu.roll(v, PY - 1, 0))
            beside = beside + jnp.where(lane == 0, 0.0, pltpu.roll(v, 1, 1))
            beside = beside + jnp.where(lane == PX - 1, 0.0, pltpu.roll(v, PX - 1, 1))
            coupled = gains[c * COMP, layer] * centre[0]
            for d in range(1, COMP):
                coupled = coupled + gains[c * COMP + d, layer] * centre[d]
            result.append(coupled - beside)
        return result

    def take(src, layer):
        return [src[c, layer] for c in range(COMP)]

    def put(dst, layer, values):
        for c in range(COMP):
            dst[c, layer] = values[c]

    def apply_at(src, layer, below=True, above=True):
        centre = take(src, layer)
        result = within(centre, layer)
        for c in range(COMP):
            if below:
                result[c] = result[c] - src[c, layer - 1]
            if above:
                result[c] = result[c] - src[c, layer + 1]
        return centre, [value * inv_row for value in result]

    def layers(lo, hi, body):
        @pl.loop(lo, hi)
        def _(layer):
            body(layer)

    def products(sums, basis):
        out = []
        for (i, j), total in zip(PAIRS, sums):
            part = basis[i][0] * basis[j][0]
            for c in range(1, COMP):
                part = part + basis[i][c] * basis[j][c]
            out.append(total + ((part[0:8] + part[8:16]) + (part[16:24] + part[24:32])))
        return tuple(out)

    def third(layer, sums, below=True):
        a2, a3 = apply_at(v2, layer, below=below)
        put(v3, layer - H, a3)
        return products(sums, (take(v0, layer), take(v1, layer), a2, a3))

    def across(sums):
        mine = [cross_high * value for value in take(v2, LAST)]
        out = list(sums)
        for i, source in enumerate((v0, v1, v2)):
            part = source[0, ABOVE] * mine[0]
            for c in range(1, COMP):
                part = part + source[c, ABOVE] * mine[c]
            n = PAIRS.index((i, 3))
            out[n] = out[n] + ((part[0:8] + part[8:16]) + (part[16:24] + part[24:32]))
        return tuple(out)

    def first(layer):
        put(v1, layer, apply_at(v0, layer)[1])

    def second(layer):
        put(v2, layer, apply_at(v1, layer)[1])

    layers(FIRST, FIRST + 2, tables_of)
    layers(LAST - 1, LAST + 1, tables_of)
    low1 = apply_at(v0, FIRST, below=False)[1]
    put(v1, FIRST, low1)
    high1 = apply_at(v0, LAST, above=False)[1]
    put(v1, LAST, high1)
    for c in range(COMP):
        w1_low[c] = low1[c]
        w1_high[c] = high1[c]
    send_w1_down.start()
    send_w1_up.start()
    first(FIRST + 1)
    first(LAST - 1)
    low2 = apply_at(v1, FIRST, below=False)[1]
    for c in range(COMP):
        w2_low[c] = low2[c]
    send_w2_down.start()
    high2 = apply_at(v1, LAST, above=False)[1]
    packed = jnp.zeros((PY, PX), jnp.float32)
    for c, value in enumerate(high2 + [mat[LAST].astype(jnp.float32)]):
        packed = jnp.where(lane == c, pltpu.roll(value, c + 1, 1), packed)
        packed = jnp.where(lane == 8 + c, pltpu.roll(value, 8 + c, 1), packed)
    pack_out[...] = packed
    send_pack_up.start()

    layers(FIRST + 2, LAST - 1, tables_of)
    layers(FIRST + 2, LAST - 1, first)
    layers(FIRST + 2, LAST - 1, second)
    sums = tuple(jnp.zeros((8, PX), jnp.float32) for _ in PAIRS)
    sums = lax.fori_loop(FIRST + 3, LAST - 2, third, sums)

    send_b_down.wait_recv()
    send_m_down.wait_recv()
    send_b_up.wait_recv()
    send_ci.wait()
    load_left = pltpu.make_async_copy(ci_left_vec, ci_left, local_sem.at[5])
    load_left.start()
    for c in range(COMP):
        v1[c, FIRST] = v1[c, FIRST] + cross_low * v0[c, BELOW]
        v1[c, LAST] = v1[c, LAST] + cross_high * v0[c, ABOVE]
    tables_of(ABOVE)
    second(FIRST + 1)
    second(LAST - 1)
    send_w1_down.wait_recv()
    send_w1_up.wait_recv()
    for c in range(COMP):
        v1[c, BELOW] = keep_low * v1[c, BELOW] + cross_low * v0[c, FIRST]
        v1[c, ABOVE] = keep_high * v1[c, ABOVE] + cross_high * v0[c, LAST]
    second(FIRST)
    second(LAST)
    sums = lax.fori_loop(FIRST + 1, FIRST + 3, third, sums)
    sums = lax.fori_loop(LAST - 2, LAST, third, sums)
    above = within(take(v0, LAST), ABOVE)
    above = [term * inv_row + v1[c, LAST] for c, term in enumerate(above)]
    sums = third(FIRST, sums, below=False)
    load_left.wait()
    send_w2_down.wait_recv()
    for c in range(COMP):
        v2[c, ABOVE] = keep_high * v2[c, ABOVE] + cross_high * above[c]
    sums = third(LAST, sums)
    sums = across(sums)
    send_pack_up.wait_recv()
    packed = pack_in[...]

    def column(c):
        return jnp.where(lane == PX - 1, pltpu.roll(packed, PX - 1 - c, 1), pltpu.roll(packed, PX - 8 - c, 1))

    at_ends = (lane == 0) | (lane == PX - 1)
    tables_of(BELOW, jnp.where(at_ends, column(COMP), 0.0).astype(jnp.int32))
    below = within(take(v0, FIRST), BELOW)
    for c in range(COMP):
        value = keep_low * column(c) + cross_low * (below[c] * inv_row + v1[c, FIRST])
        v3[c, 0] = v3[c, 0] + cross_low * jnp.where(at_ends, value, 0.0)

    for j in range(KC):
        for side, ids in ((0, ci_own), (1, ci_left)):
            spot = ids[0, j]
            c, layer, at = spot // (CZ * PY), (spot // PY) % CZ, spot % PY
            place = side * KC + j
            rows[pl.ds(place, 1), :] = v0[c, layer + H, pl.ds(at, 1), :]
            rows[pl.ds(16 + place, 1), :] = v1[c, layer + H, pl.ds(at, 1), :]
            rows[pl.ds(32 + place, 1), :] = v2[c, layer + H, pl.ds(at, 1), :]
            rows[pl.ds(48 + place, 1), :] = v3[c, layer, pl.ds(at, 1), :]
    rows[pl.ds(64, 64), :] = jnp.zeros((64, PX), jnp.float32)
    turned = jnp.transpose(rows[...])
    lane1 = lax.broadcasted_iota(jnp.int32, (1, PX), 1)
    own_row = jnp.where((lane1 // KC) % 2 == 0, turned[PX - 1 : PX, :], turned[0:1, :])
    own_row = jnp.where(lane1 < 64, own_row, 0.0)
    for n, total in enumerate(sums):
        whole = jnp.sum(jnp.sum(total, axis=0, keepdims=True), axis=1, keepdims=True)
        own_row = jnp.where(lane1 == 64 + n, whole, own_row)
    send_row[...] = own_row
    ex[pl.ds(inn, 1), :] = own_row
    for k in range(1, N_IN):
        remote(send_row, ex.at[pl.ds(inn, 1)], send_sem.at[8], recv_sem.at[8], in_peer(k)).start()
    everything = ex.at[pl.ds(0, N_IN - 1)]
    remote(everything, everything, send_sem.at[8], recv_sem.at[8], in_peer(1)).wait()

    everyone = ex[...]
    total = jnp.sum(everyone, axis=0, keepdims=True)
    gram = {}
    for n, (i, j) in enumerate(PAIRS):
        value = jnp.sum(jnp.where(lane1 == 64 + n, total, 0.0), axis=1, keepdims=True)
        gram[i, j] = gram[j, i] = value

    def form(p, q, offset):
        value = None
        for i, a in enumerate(p):
            for j, b in enumerate(q):
                term = a * b * gram[i, j + offset]
                value = term if value is None else value + term
        return value

    res = [jnp.ones((1, 1), jnp.float32)]
    direction, previous = list(res), []
    rr = form(res, res, 0)
    dd, beta = rr, None
    answer = [jnp.zeros((1, 1), jnp.float32) for _ in range(ITERS)]
    for step in range(ITERS):
        delta = width * form(direction, direction, 1)
        if step:
            delta = delta + sigma * (beta * beta * dd_before)
        inverse = 1.0 / (sigma * rr + delta)
        alpha = rr * inverse
        for j, value in enumerate(direction):
            answer[j] = answer[j] + alpha * value
        moved = []
        for j in range(step + 2):
            value = None
            if j <= step:
                value = res[j] * delta
                if j < len(previous):
                    value = value - sigma * rr * (beta * previous[j])
                value = value * inverse
            if j:
                part = (alpha * width) * direction[j - 1]
                value = -part if value is None else value - part
            moved.append(value)
        if step + 1 < ITERS:
            new = form(moved, moved, 0)
            beta = new / rr
            previous = direction
            direction = [
                value + beta * direction[j] if j <= step else value for j, value in enumerate(moved)
            ]
            dd_before = dd
            dd = new + beta * beta * dd
            rr = new
        res = moved

    factors = jnp.zeros((1, PX), jnp.float32)
    for k in range(ITERS + 1):
        factors = jnp.where(lane1 // 16 == k, res[k], factors)
    mixed = everyone * factors
    mixed = (mixed + pltpu.roll(mixed, PX - 16, 1)) + (pltpu.roll(mixed, PX - 32, 1) + pltpu.roll(mixed, PX - 48, 1))
    unit = jnp.zeros((1, PX), jnp.float32)
    for i in range(N_IN):
        piece = mixed[i : i + 1, :]
        piece = jnp.where(lane1 < 8, piece, 0.0) + pltpu.roll(jnp.where((lane1 >= 8) & (lane1 < 16), piece, 0.0), 56, 1)
        unit = unit + (pltpu.roll(piece, KC * i, 1) if i else piece)

    spot_row = y * 16 + zl * 2 + core
    ag[pl.ds(spot_row, 1), :] = unit
    mine = ag.at[pl.ds(spot_row, 1)]
    z_peers = [z_peer(d, o) for d in (0,) + ZSTEPS for o in (0, 1) if d or o]
    for peer in z_peers:
        remote(mine, mine, send_sem.at[9], recv_sem.at[9], peer).start()

    wide = [jnp.broadcast_to(value, (1, PX)) for value in res]
    wide_x = [jnp.broadcast_to(value, (1, PX)) for value in answer]

    def finish(layer, faces):
        for c in range(COMP):
            a0, a1, a2, a3 = v0[c, layer + H], v1[c, layer + H], v2[c, layer + H], v3[c, layer]
            sol_out[c, layer] = wide_x[0] * a0 + wide_x[1] * a1 + wide_x[2] * a2
            left = (wide[0] * a0 + wide[1] * a1) + (wide[2] * a2 + wide[3] * a3)
            place = c * CZ + layer
            faces = jnp.where(lane == place, pltpu.roll(left, place + 1, 1), faces)
            faces = jnp.where(lane == place + 32, pltpu.roll(left, place + 32, 1), faces)
        return faces

    faces = lax.fori_loop(0, CZ, finish, jnp.zeros((PY, PX), jnp.float32))
    faces = jnp.transpose(jnp.concatenate([faces, jnp.zeros((PX - PY, PX), jnp.float32)], axis=0))
    left_out[...] = faces[32:64, :]
    left_copy = remote(left_out, left_in, send_sem.at[11], recv_sem.at[11], sub_prev)
    left_copy.start()

    arrived = ag.at[pl.ds(0, len(z_peers))]
    remote(arrived, arrived, send_sem.at[9], recv_sem.at[9], in_peer(1)).wait()
    mine = ag.at[pl.ds(y * 16, 12)]
    for k in range(1, NY):
        remote(mine, mine, send_sem.at[10], recv_sem.at[10], y_peer(k)).start()
    load_inv.wait()
    left_copy.wait()
    summed = faces[0:32, :] + left_in[...]
    for copy in halos[:-1]:
        copy.wait_send()
    arrived = ag.at[pl.ds(0, 12 * (NY - 1))]
    remote(arrived, arrived, send_sem.at[10], recv_sem.at[10], in_peer(1)).wait()

    lane8 = lax.broadcasted_iota(jnp.int32, (8, PX), 1)
    row8 = lax.broadcasted_iota(jnp.int32, (8, PX), 0)
    even = [ag[pl.ds(k * 2, NY, stride=16), :] for k in range(NZL)]
    odd = [ag[pl.ds(k * 2 + 1, NY, stride=16), :] for k in range(NZL)]
    turned_even = [pltpu.roll(value, NY - 1, 0) for value in even]
    acc = jnp.zeros((KC, PX), jnp.float32)
    for k in range(NZL):
        after = jnp.where(row8 == NY - 1, turned_even[(k + 1) % NZL], turned_even[k])
        block = jnp.where(lane8 < 64, even[k], after) + pltpu.roll(odd[k], 64, 1)
        for at in range(NY):
            column = (k * NY + at) * PX
            acc = acc + cinv[:, column : column + PX] * block[at : at + 1, :]
    coarse = jnp.sum(acc, axis=1, keepdims=True)
    spots = row * PY + lane
    for j in range(KC):
        hit = (spots == ci_own[0, j]) & (lane < PY)
        summed = summed + jnp.where(hit, coarse[j : j + 1, :], 0.0)
    for c in range(COMP):
        face_out[0, c] = summed[c * CZ : (c + 1) * CZ, 0:PY]


def on_device(body_load, materials, material_tables, corner_index, coarse_inverse):
    f32, i32 = jnp.float32, jnp.int32
    anywhere = pl.BlockSpec(memory_space=pl.ANY)
    vmem = pl.BlockSpec(memory_space=pltpu.VMEM)
    layer = (COMP, PY, PX)
    return pl.pallas_call(
        kernel,
        out_shape=(
            pltpu.VMEM((COMP, CZ, PY, PX), f32),
            pltpu.VMEM((1, COMP, CZ, PY), f32),
        ),
        in_specs=[anywhere] * 5,
        out_specs=(vmem, vmem),
        scratch_shapes=[
            pltpu.VMEM((COMP, EXT, PY, PX), f32),
            pltpu.VMEM((COMP, EXT, PY, PX), f32),
            pltpu.VMEM((COMP, EXT, PY, PX), f32),
            pltpu.VMEM((COMP, CZ, PY, PX), f32),
            pltpu.VMEM((EXT, PY, PX), i32),
            pltpu.VMEM((COMP * COMP, EXT, PY, PX), f32),
            pltpu.VMEM(layer, f32),
            pltpu.VMEM(layer, f32),
            pltpu.VMEM(layer, f32),
            pltpu.VMEM((PY, PX), f32),
            pltpu.VMEM((PY, PX), f32),
            pltpu.VMEM((KC, N_SUB * N_IN * KC), f32),
            pltpu.VMEM((PX, PX), f32),
            pltpu.VMEM((1, PX), f32),
            pltpu.VMEM((N_IN, PX), f32),
            pltpu.VMEM((NY * 16, PX), f32),
            pltpu.VMEM((PY, PX), f32),
            pltpu.VMEM((PY, PX), f32),
            pltpu.VMEM((1, KC), i32),
            pltpu.VMEM((1, KC), i32),
            pltpu.SMEM((1, KC), i32),
            pltpu.SMEM((1, KC), i32),
            pltpu.SMEM((COMP, COMP, NMAT), f32),
            pltpu.SemaphoreType.DMA((7,)),
            pltpu.SemaphoreType.DMA((12,)),
            pltpu.SemaphoreType.DMA((12,)),
        ],
        compiler_params=pltpu.CompilerParams(collective_id=0, has_side_effects=True),
    )(
        body_load,
        materials,
        jnp.transpose(material_tables, (1, 2, 0)),
        corner_index.reshape(1, KC),
        coarse_inverse,
    )


def solution(mesh):
    return jax.shard_map(
        on_device,
        mesh=mesh,
        in_specs=(
            P(None, "in", None, "sub"),
            P("in", None, "sub"),
            P(),
            P(("sub", "in")),
            P(("sub", "in"), None),
        ),
        out_specs=(P(None, "in", None, "sub"), P("sub", None, "in", None)),
        check_vma=False,
    )
```

time: 79.4 us -> 66.3 us (0.84)
  Pallas kernels: 74.6 us -> 64.2 us
  local copies, waits for them, and re-layouts: 3.88 us -> 1.4 us
    pallas_call x1, Pallas kernels: 74.6 us -> 64.2 us  [on_device(): pl.pallas_call(kernel, out_shape=(pltpu.VMEM((COMP, CZ, PY, PX), f32), pl...]
    unnamed x5 -> x2, local copies, waits for them, and re-layouts: 3.88 us -> 1.4 us
where the time goes in v2:
time: 66.3 us; the launch traced here: 66.2 us
  Pallas kernels  64.2 us (97%)
  local copies, waits for them, and re-layouts  1.4 us (2%)
    pallas_call x1, Pallas kernels, on_device(): pl.pallas_call(kernel, out_shape=(pltpu.VMEM((COMP, CZ, PY, PX), f32), pl...  64.2 us
    unnamed x2, local copies, waits for them, and re-layouts  1.4 us

profile of v2, /device:TPU:1, one launch (start us, length us, event | category | flops | bytes accessed | tf_op | source)
XLA Modules:
  0.0 66.2 jit_solution(6323509670994318332)
XLA Ops:
  0.6 64.2 %shard_map.68 = (f32[4,8,32,128]{3,2,1,0:T(8,128)S(1)}, f32[1,4,8,32]{3,2,1,0:T(8,128)S(1)}) custom-call(f32[4,8,32,128]{3,2,1,0:T(8,128)} %b_hbm.1, s32[8,32,128]{2,1,0:T(8,128)} %m_hbm.1, f32[4,4,8]{2,1,0:T(4,128)} %bitcast.2, s32[1,8]{1,0:T(1,128)} %bitcast.3, f32[8,6144]{1,0:T(8,128)} %cinv_hbm.1), custom_call_target="tpu_custom_call" | custom-call | tf_op jit(solution)/shard_map/pallas_call | solution.py:415
  64.8 0.8 %copy.9 = f32[4,8,32,128]{3,2,1,0:T(8,128)} copy(f32[4,8,32,128]{3,2,1,0:T(8,128)S(1)} %get-tuple-element.2) | data formatting | bytes 1048576
  65.6 0.6 copy.10

commit v3 on v2

--- a/solution.py
+++ b/solution.py
@@ -12,9 +12,8 @@
 H = 1
 EXT = CZ + 2 * H
 FIRST, LAST, BELOW, ABOVE = H, H + CZ - 1, 0, H + CZ
-NY, NZL = 8, 6
+NX_CHIPS, NY, NZL = 4, 8, 6
 PAIRS = [(0, 0), (0, 1), (0, 2), (0, 3), (1, 1), (1, 2), (1, 3), (2, 2), (2, 3)]
-ZSTEPS = (1, 2, 3, 10, 11)
 
 
 def remote(src, dst, send, recv, device):
@@ -26,7 +25,7 @@
 def kernel(
     b_hbm, m_hbm, tab_hbm, ci_hbm, cinv_hbm,
     sol_out, face_out,
-    v0, v1, v2, v3, mat, gains, w1_low, w1_high, w2_low, pack_out, pack_in,
+    v0, v1, v2, v3, relay, mat, gains, w1_low, w1_high, w2_low, w2_in, pack_out, pack_in,
     cinv, rows, send_row, ex, ag, left_out, left_in,
     ci_vec, ci_left_vec, ci_own, ci_left, tab, local_sem, send_sem, recv_sem,
 ):
@@ -34,26 +33,23 @@
     core, y, zl = sub % 2, (sub // 2) % NY, sub // (2 * NY)
     x, z = inn // 2, (inn % 2) * NZL + zl
 
-    def device(core_, y_, z_):
-        return {"sub": ((z_ % NZL) * NY + y_) * 2 + core_, "in": x * 2 + z_ // NZL}
-
     def in_peer(k):
         return {"sub": sub, "in": (inn + k) % N_IN}
 
-    def z_peer(d, other):
-        return device((core + other) % 2, y, (z + d) % (2 * NZL))
-
-    def y_peer(k):
-        return device(core, (y + k) % NY, z)
+    def plane_peer(dx, dz):
+        z_ = (z + dz) % (2 * NZL)
+        return {"sub": ((z_ % NZL) * NY + y) * 2 + core, "in": ((x + dx) % NX_CHIPS) * 2 + z_ // NZL}
+
+    def y_peer(k, other):
+        return {"sub": (zl * NY + (y + k) % NY) * 2 + (core + other) % 2, "in": inn}
 
     sub_next = {"sub": (sub + 1) % N_SUB, "in": inn}
     sub_prev = {"sub": (sub + N_SUB - 1) % N_SUB, "in": inn}
 
     barrier = pltpu.get_barrier_semaphore()
-    greet = [in_peer(k) for k in (1, N_IN - 1)]
-    greet += [in_peer(k) for k in range(2, N_IN - 1)]
-    greet += [z_peer(d, o) for d in (0, 1, 2, 3, 9, 10, 11) for o in (0, 1) if d or o]
-    greet += [y_peer(k) for k in range(1, NY)]
+    greet = [in_peer(1), in_peer(N_IN - 1)]
+    greet += [plane_peer(dx, dz) for dz in range(2 * NZL) for dx in range(NX_CHIPS) if dx or dz]
+    greet += [y_peer(k, o) for k in range(NY) for o in (0, 1) if k or o]
     greet += [sub_next, sub_prev]
     for peer in greet:
         pl.semaphore_signal(barrier, inc=1, device_id=peer, device_id_type=MESH)
@@ -100,12 +96,40 @@
     send_m_down = remote(mat.at[FIRST], mat.at[ABOVE], send_sem.at[2], recv_sem.at[2], down)
     send_w1_up = remote(w1_high, v1.at[:, BELOW], send_sem.at[3], recv_sem.at[3], up)
     send_w1_down = remote(w1_low, v1.at[:, ABOVE], send_sem.at[4], recv_sem.at[4], down)
-    send_w2_down = remote(w2_low, v2.at[:, ABOVE], send_sem.at[5], recv_sem.at[5], down)
+    send_w2_down = remote(w2_low, w2_in, send_sem.at[5], recv_sem.at[5], down)
     send_pack_up = remote(pack_out, pack_in, send_sem.at[6], recv_sem.at[6], up)
     send_ci = remote(ci_vec, ci_left_vec, send_sem.at[7], recv_sem.at[7], sub_next)
-    halos = (send_b_up, send_b_down, send_m_down, send_w1_up, send_w1_down, send_w2_down, send_pack_up, send_ci)
-    for copy in (send_b_down, send_b_up, send_m_down, send_ci):
-        copy.start()
+    up_relayed, up_via, down_relayed, down_via = N_IN - 3, N_IN - 1, 2, 0
+    has_up, has_down = inn < N_IN - 1, inn > 0
+
+    def to(index):
+        return {"sub": sub, "in": index}
+
+    relay_up = remote(v0.at[:, LAST], relay, send_sem.at[0], recv_sem.at[11], to(up_via))
+    relay_down = remote(v0.at[:, FIRST], relay, send_sem.at[1], recv_sem.at[11], to(down_via))
+    pass_up = remote(relay, v0.at[:, BELOW], send_sem.at[11], recv_sem.at[0], to(up_relayed + 1))
+    pass_down = remote(relay, v0.at[:, ABOVE], send_sem.at[11], recv_sem.at[1], to(down_relayed - 1))
+    pl.when(inn == down_relayed)(relay_down.start)
+    pl.when(inn == up_relayed)(relay_up.start)
+    pl.when(has_down & (inn != down_relayed))(send_b_down.start)
+    pl.when(has_up & (inn != up_relayed))(send_b_up.start)
+    pl.when(has_down)(send_m_down.start)
+    send_ci.start()
+
+    @pl.when(inn == 0)
+    def _():
+        for c in range(COMP):
+            v0[c, BELOW] = jnp.zeros((PY, PX), jnp.float32)
+            v1[c, BELOW] = jnp.zeros((PY, PX), jnp.float32)
+        pack_in[...] = jnp.zeros((16, PX), jnp.float32)
+
+    @pl.when(inn == N_IN - 1)
+    def _():
+        mat[ABOVE] = jnp.zeros((PY, PX), jnp.int32)
+        for c in range(COMP):
+            v0[c, ABOVE] = jnp.zeros((PY, PX), jnp.float32)
+            v1[c, ABOVE] = jnp.zeros((PY, PX), jnp.float32)
+            w2_in[c] = jnp.zeros((PY, PX), jnp.float32)
 
     lane = lax.broadcasted_iota(jnp.int32, (PY, PX), 1)
     row = lax.broadcasted_iota(jnp.int32, (PY, PX), 0)
@@ -155,9 +179,12 @@
         def _(layer):
             body(layer)
 
-    def products(sums, basis):
+    def products(sums, basis, only=None):
         out = []
         for (i, j), total in zip(PAIRS, sums):
+            if basis[j] is None or only not in (None, j):
+                out.append(total)
+                continue
             part = basis[i][0] * basis[j][0]
             for c in range(1, COMP):
                 part = part + basis[i][c] * basis[j][c]
@@ -195,21 +222,22 @@
     for c in range(COMP):
         w1_low[c] = low1[c]
         w1_high[c] = high1[c]
-    send_w1_down.start()
-    send_w1_up.start()
+    pl.when(has_down)(send_w1_down.start)
+    pl.when(has_up)(send_w1_up.start)
     first(FIRST + 1)
     first(LAST - 1)
     low2 = apply_at(v1, FIRST, below=False)[1]
     for c in range(COMP):
         w2_low[c] = low2[c]
-    send_w2_down.start()
+    pl.when(has_down)(send_w2_down.start)
     high2 = apply_at(v1, LAST, above=False)[1]
     packed = jnp.zeros((PY, PX), jnp.float32)
     for c, value in enumerate(high2 + [mat[LAST].astype(jnp.float32)]):
         packed = jnp.where(lane == c, pltpu.roll(value, c + 1, 1), packed)
         packed = jnp.where(lane == 8 + c, pltpu.roll(value, 8 + c, 1), packed)
-    pack_out[...] = packed
-    send_pack_up.start()
+    blank = jnp.zeros((PX - PY, PX), jnp.float32)
+    pack_out[...] = jnp.transpose(jnp.concatenate([packed, blank], axis=0))[0:16, :]
+    pl.when(has_up)(send_pack_up.start)
 
     layers(FIRST + 2, LAST - 1, tables_of)
     layers(FIRST + 2, LAST - 1, first)
@@ -217,9 +245,19 @@
     sums = tuple(jnp.zeros((8, PX), jnp.float32) for _ in PAIRS)
     sums = lax.fori_loop(FIRST + 3, LAST - 2, third, sums)
 
-    send_b_down.wait_recv()
-    send_m_down.wait_recv()
-    send_b_up.wait_recv()
+    @pl.when(inn == up_via)
+    def _():
+        relay_up.wait_recv()
+        pass_up.start()
+
+    @pl.when(inn == down_via)
+    def _():
+        relay_down.wait_recv()
+        pass_down.start()
+
+    pl.when(has_up)(send_b_down.wait_recv)
+    pl.when(has_up)(send_m_down.wait_recv)
+    pl.when(has_down)(send_b_up.wait_recv)
     send_ci.wait()
     load_left = pltpu.make_async_copy(ci_left_vec, ci_left, local_sem.at[5])
     load_left.start()
@@ -229,8 +267,8 @@
     tables_of(ABOVE)
     second(FIRST + 1)
     second(LAST - 1)
-    send_w1_down.wait_recv()
-    send_w1_up.wait_recv()
+    pl.when(has_up)(send_w1_down.wait_recv)
+    pl.when(has_down)(send_w1_up.wait_recv)
     for c in range(COMP):
         v1[c, BELOW] = keep_low * v1[c, BELOW] + cross_low * v0[c, FIRST]
         v1[c, ABOVE] = keep_high * v1[c, ABOVE] + cross_high * v0[c, LAST]
@@ -242,13 +280,9 @@
     above = [term * inv_row + v1[c, LAST] for c, term in enumerate(above)]
     sums = third(FIRST, sums, below=False)
     load_left.wait()
-    send_w2_down.wait_recv()
-    for c in range(COMP):
-        v2[c, ABOVE] = keep_high * v2[c, ABOVE] + cross_high * above[c]
-    sums = third(LAST, sums)
-    sums = across(sums)
-    send_pack_up.wait_recv()
-    packed = pack_in[...]
+    pl.when(has_down)(send_pack_up.wait_recv)
+    packed = jnp.concatenate([pack_in[...], jnp.zeros((PX - 16, PX), jnp.float32)], axis=0)
+    packed = jnp.transpose(packed)[0:PY, :]
 
     def column(c):
         return jnp.where(lane == PX - 1, pltpu.roll(packed, PX - 1 - c, 1), pltpu.roll(packed, PX - 8 - c, 1))
@@ -260,35 +294,63 @@
         value = keep_low * column(c) + cross_low * (below[c] * inv_row + v1[c, FIRST])
         v3[c, 0] = v3[c, 0] + cross_low * jnp.where(at_ends, value, 0.0)
 
+    places = []
     for j in range(KC):
         for side, ids in ((0, ci_own), (1, ci_left)):
             spot = ids[0, j]
             c, layer, at = spot // (CZ * PY), (spot // PY) % CZ, spot % PY
             place = side * KC + j
+            places.append((place, c, layer, at))
             rows[pl.ds(place, 1), :] = v0[c, layer + H, pl.ds(at, 1), :]
             rows[pl.ds(16 + place, 1), :] = v1[c, layer + H, pl.ds(at, 1), :]
             rows[pl.ds(32 + place, 1), :] = v2[c, layer + H, pl.ds(at, 1), :]
-            rows[pl.ds(48 + place, 1), :] = v3[c, layer, pl.ds(at, 1), :]
     rows[pl.ds(64, 64), :] = jnp.zeros((64, PX), jnp.float32)
+    lane1 = lax.broadcasted_iota(jnp.int32, (1, PX), 1)
+
+    def with_sums(into, chosen):
+        for n, (i, j) in enumerate(PAIRS):
+            if chosen(j):
+                whole = jnp.sum(jnp.sum(sums[n], axis=0, keepdims=True), axis=1, keepdims=True)
+                into = jnp.where(lane1 == 64 + n, whole, into)
+        return into
+
+    a2 = take(v2, LAST)
+    a0, a1 = take(v0, LAST), take(v1, LAST)
+    sums = products(sums, (a0, a1, a2, None))
+    sums_row = with_sums(jnp.zeros((1, PX), jnp.float32), lambda j: j < 3)
+    pl.when(has_up)(send_w2_down.wait_recv)
+    for c in range(COMP):
+        v2[c, ABOVE] = keep_high * w2_in[c] + cross_high * above[c]
+    a3 = apply_at(v2, LAST)[1]
+    put(v3, LAST - H, a3)
+    sums = products(sums, (a0, a1, a2, a3), only=3)
+    sums = across(sums)
+    for place, c, layer, at in places:
+        rows[pl.ds(48 + place, 1), :] = v3[c, layer, pl.ds(at, 1), :]
     turned = jnp.transpose(rows[...])
-    lane1 = lax.broadcasted_iota(jnp.int32, (1, PX), 1)
     own_row = jnp.where((lane1 // KC) % 2 == 0, turned[PX - 1 : PX, :], turned[0:1, :])
-    own_row = jnp.where(lane1 < 64, own_row, 0.0)
-    for n, total in enumerate(sums):
-        whole = jnp.sum(jnp.sum(total, axis=0, keepdims=True), axis=1, keepdims=True)
-        own_row = jnp.where(lane1 == 64 + n, whole, own_row)
+    own_row = jnp.where(lane1 < 64, own_row, with_sums(sums_row, lambda j: j == 3))
     send_row[...] = own_row
-    ex[pl.ds(inn, 1), :] = own_row
-    for k in range(1, N_IN):
-        remote(send_row, ex.at[pl.ds(inn, 1)], send_sem.at[8], recv_sem.at[8], in_peer(k)).start()
-    everything = ex.at[pl.ds(0, N_IN - 1)]
-    remote(everything, everything, send_sem.at[8], recv_sem.at[8], in_peer(1)).wait()
-
-    everyone = ex[...]
-    total = jnp.sum(everyone, axis=0, keepdims=True)
+    ex[pl.ds(zl * N_IN + inn, 1), :] = own_row
+    n_plane = 2 * NZL * NX_CHIPS
+    for dz in range(2 * NZL):
+        for dx in range(NX_CHIPS):
+            if dx or dz:
+                spot = ex.at[pl.ds(zl * N_IN + inn, 1)]
+                remote(send_row, spot, send_sem.at[8], recv_sem.at[8], plane_peer(dx, dz)).start()
+    arrived = ex.at[pl.ds(0, n_plane - 1)]
+    remote(arrived, arrived, send_sem.at[8], recv_sem.at[8], in_peer(1)).wait()
+
+    lane8 = lax.broadcasted_iota(jnp.int32, (8, PX), 1)
+    row8 = lax.broadcasted_iota(jnp.int32, (8, PX), 0)
+    everyone = [ex[pl.ds(k * N_IN, N_IN), :] for k in range(NZL)]
+    total = None
+    for k in reversed(range(NZL)):
+        part = jnp.sum(everyone[k], axis=0, keepdims=True)
+        total = jnp.broadcast_to(part, (8, PX)) if total is None else jnp.where(row8 == k, part, total)
     gram = {}
     for n, (i, j) in enumerate(PAIRS):
-        value = jnp.sum(jnp.where(lane1 == 64 + n, total, 0.0), axis=1, keepdims=True)
+        value = jnp.sum(jnp.where(lane8 == 64 + n, total, 0.0), axis=1, keepdims=True)
         gram[i, j] = gram[j, i] = value
 
     def form(p, q, offset):
@@ -299,11 +361,11 @@
                 value = term if value is None else value + term
         return value
 
-    res = [jnp.ones((1, 1), jnp.float32)]
+    res = [jnp.ones((8, 1), jnp.float32)]
     direction, previous = list(res), []
     rr = form(res, res, 0)
     dd, beta = rr, None
-    answer = [jnp.zeros((1, 1), jnp.float32) for _ in range(ITERS)]
+    answer = [jnp.zeros((8, 1), jnp.float32) for _ in range(ITERS)]
     for step in range(ITERS):
         delta = width * form(direction, direction, 1)
         if step:
@@ -336,60 +398,73 @@
             rr = new
         res = moved
 
-    factors = jnp.zeros((1, PX), jnp.float32)
+    factors = jnp.zeros((8, PX), jnp.float32)
     for k in range(ITERS + 1):
-        factors = jnp.where(lane1 // 16 == k, res[k], factors)
-    mixed = everyone * factors
-    mixed = (mixed + pltpu.roll(mixed, PX - 16, 1)) + (pltpu.roll(mixed, PX - 32, 1) + pltpu.roll(mixed, PX - 48, 1))
-    unit = jnp.zeros((1, PX), jnp.float32)
-    for i in range(N_IN):
-        piece = mixed[i : i + 1, :]
-        piece = jnp.where(lane1 < 8, piece, 0.0) + pltpu.roll(jnp.where((lane1 >= 8) & (lane1 < 16), piece, 0.0), 56, 1)
-        unit = unit + (pltpu.roll(piece, KC * i, 1) if i else piece)
-
-    spot_row = y * 16 + zl * 2 + core
-    ag[pl.ds(spot_row, 1), :] = unit
-    mine = ag.at[pl.ds(spot_row, 1)]
-    z_peers = [z_peer(d, o) for d in (0,) + ZSTEPS for o in (0, 1) if d or o]
-    for peer in z_peers:
-        remote(mine, mine, send_sem.at[9], recv_sem.at[9], peer).start()
-
-    wide = [jnp.broadcast_to(value, (1, PX)) for value in res]
-    wide_x = [jnp.broadcast_to(value, (1, PX)) for value in answer]
-
-    def finish(layer, faces):
+        factors = jnp.where(lane8 // 16 == k, res[k], factors)
+    units = jnp.zeros((8, PX), jnp.float32)
+    for k in range(NZL):
+        mixed = everyone[k] * factors[k : k + 1, :]
+        mixed = (mixed + pltpu.roll(mixed, PX - 16, 1)) + (
+            pltpu.roll(mixed, PX - 32, 1) + pltpu.roll(mixed, PX - 48, 1)
+        )
+        mixed = jnp.where(lane8 < 8, mixed, 0.0) + pltpu.roll(
+            jnp.where((lane8 >= 8) & (lane8 < 16), mixed, 0.0), 56, 1
+        )
+        mixed = pltpu.roll(mixed, 0, 1, stride=KC, stride_axis=0)
+        units = jnp.where(row8 == k, jnp.sum(mixed, axis=0, keepdims=True), units)
+    spot_row = pl.multiple_of(y * 16 + core * 8, 8)
+    ag[pl.ds(spot_row, 8), :] = units
+    mine = ag.at[pl.ds(spot_row, 8)]
+    for k in range(NY):
+        for o in (0, 1):
+            if k or o:
+                remote(mine, mine, send_sem.at[9], recv_sem.at[9], y_peer(k, o)).start()
+
+    def own_of(value):
+        value = jnp.sum(jnp.where(row8 == zl, value, 0.0), axis=0, keepdims=True)
+        return value
+
+    wide = [own_of(value) for value in res]
+    wide_x = [own_of(value) for value in answer]
+
+    def face_of(layer, faces):
         for c in range(COMP):
             a0, a1, a2, a3 = v0[c, layer + H], v1[c, layer + H], v2[c, layer + H], v3[c, layer]
-            sol_out[c, layer] = wide_x[0] * a0 + wide_x[1] * a1 + wide_x[2] * a2
             left = (wide[0] * a0 + wide[1] * a1) + (wide[2] * a2 + wide[3] * a3)
             place = c * CZ + layer
             faces = jnp.where(lane == place, pltpu.roll(left, place + 1, 1), faces)
             faces = jnp.where(lane == place + 32, pltpu.roll(left, place + 32, 1), faces)
         return faces
 
-    faces = lax.fori_loop(0, CZ, finish, jnp.zeros((PY, PX), jnp.float32))
+    faces = lax.fori_loop(0, CZ, face_of, jnp.zeros((PY, PX), jnp.float32))
     faces = jnp.transpose(jnp.concatenate([faces, jnp.zeros((PX - PY, PX), jnp.float32)], axis=0))
     left_out[...] = faces[32:64, :]
-    left_copy = remote(left_out, left_in, send_sem.at[11], recv_sem.at[11], sub_prev)
+    left_copy = remote(left_out, left_in, send_sem.at[10], recv_sem.at[10], sub_prev)
     left_copy.start()
 
-    arrived = ag.at[pl.ds(0, len(z_peers))]
-    remote(arrived, arrived, send_sem.at[9], recv_sem.at[9], in_peer(1)).wait()
-    mine = ag.at[pl.ds(y * 16, 12)]
-    for k in range(1, NY):
-        remote(mine, mine, send_sem.at[10], recv_sem.at[10], y_peer(k)).start()
+    def solve_of(layer):
+        for c in range(COMP):
+            a0, a1, a2 = v0[c, layer + H], v1[c, layer + H], v2[c, layer + H]
+            sol_out[c, layer] = wide_x[0] * a0 + wide_x[1] * a1 + wide_x[2] * a2
+
+    layers(0, CZ, solve_of)
     load_inv.wait()
     left_copy.wait()
     summed = faces[0:32, :] + left_in[...]
-    for copy in halos[:-1]:
-        copy.wait_send()
-    arrived = ag.at[pl.ds(0, 12 * (NY - 1))]
-    remote(arrived, arrived, send_sem.at[10], recv_sem.at[10], in_peer(1)).wait()
-
-    lane8 = lax.broadcasted_iota(jnp.int32, (8, PX), 1)
-    row8 = lax.broadcasted_iota(jnp.int32, (8, PX), 0)
-    even = [ag[pl.ds(k * 2, NY, stride=16), :] for k in range(NZL)]
-    odd = [ag[pl.ds(k * 2 + 1, NY, stride=16), :] for k in range(NZL)]
+    pl.when(has_up)(send_b_up.wait_send)
+    pl.when(has_down)(send_b_down.wait_send)
+    pl.when(has_down)(send_m_down.wait_send)
+    pl.when(has_up)(send_w1_up.wait_send)
+    pl.when(has_down)(send_w1_down.wait_send)
+    pl.when(has_down)(send_w2_down.wait_send)
+    pl.when(has_up)(send_pack_up.wait_send)
+    pl.when(inn == up_via)(pass_up.wait_send)
+    pl.when(inn == down_via)(pass_down.wait_send)
+    arrived = ag.at[pl.ds(0, 8 * (2 * NY - 1))]
+    remote(arrived, arrived, send_sem.at[9], recv_sem.at[9], in_peer(1)).wait()
+
+    even = [ag[pl.ds(k, NY, stride=16), :] for k in range(NZL)]
+    odd = [ag[pl.ds(8 + k, NY, stride=16), :] for k in range(NZL)]
     turned_even = [pltpu.roll(value, NY - 1, 0) for value in even]
     acc = jnp.zeros((KC, PX), jnp.float32)
     for k in range(NZL):
@@ -425,17 +500,19 @@
             pltpu.VMEM((COMP, EXT, PY, PX), f32),
             pltpu.VMEM((COMP, EXT, PY, PX), f32),
             pltpu.VMEM((COMP, CZ, PY, PX), f32),
+            pltpu.VMEM(layer, f32),
             pltpu.VMEM((EXT, PY, PX), i32),
             pltpu.VMEM((COMP * COMP, EXT, PY, PX), f32),
             pltpu.VMEM(layer, f32),
             pltpu.VMEM(layer, f32),
             pltpu.VMEM(layer, f32),
-            pltpu.VMEM((PY, PX), f32),
-            pltpu.VMEM((PY, PX), f32),
+            pltpu.VMEM(layer, f32),
+            pltpu.VMEM((16, PX), f32),
+            pltpu.VMEM((16, PX), f32),
             pltpu.VMEM((KC, N_SUB * N_IN * KC), f32),
             pltpu.VMEM((PX, PX), f32),
             pltpu.VMEM((1, PX), f32),
-            pltpu.VMEM((N_IN, PX), f32),
+            pltpu.VMEM((NZL * N_IN, PX), f32),
             pltpu.VMEM((NY * 16, PX), f32),
             pltpu.VMEM((PY, PX), f32),
             pltpu.VMEM((PY, PX), f32),

time: 66.3 us -> 63.4 us (0.956)
  Pallas kernels: 64.2 us -> 61.2 us
    pallas_call x1, Pallas kernels: 64.2 us -> 61.2 us  [on_device(): pl.pallas_call(kernel, out_shape=(pltpu.VMEM((COMP, CZ, PY, PX), f32), pl...]
where the time goes in v3:
time: 63.4 us; the launch traced here: 63.3 us
  Pallas kernels  61.2 us (97%)
  local copies, waits for them, and re-layouts  1.4 us (2%)
  between operations  0.64 us (1%)
    pallas_call x1, Pallas kernels, on_device(): pl.pallas_call(kernel, out_shape=(pltpu.VMEM((COMP, CZ, PY, PX), f32), pl...  61.2 us
    unnamed x2, local copies, waits for them, and re-layouts  1.4 us

profile of v3, /device:TPU:1, one launch (start us, length us, event | category | flops | bytes accessed | tf_op | source)
XLA Modules:
  0.0 63.3 jit_solution(9687219755358146325)
XLA Ops:
  0.6 61.2 %shard_map.68 = (f32[4,8,32,128]{3,2,1,0:T(8,128)S(1)}, f32[1,4,8,32]{3,2,1,0:T(8,128)S(1)}) custom-call(f32[4,8,32,128]{3,2,1,0:T(8,128)} %b_hbm.1, s32[8,32,128]{2,1,0:T(8,128)} %m_hbm.1, f32[4,4,8]{2,1,0:T(4,128)} %bitcast.2, s32[1,8]{1,0:T(1,128)} %bitcast.3, f32[8,6144]{1,0:T(8,128)} %cinv_hbm.1), custom_call_target="tpu_custom_call" | custom-call | tf_op jit(solution)/shard_map/pallas_call | solution.py:490
  61.8 0.8 %copy.9 = f32[4,8,32,128]{3,2,1,0:T(8,128)} copy(f32[4,8,32,128]{3,2,1,0:T(8,128)S(1)} %get-tuple-element.2) | data formatting | bytes 1048576
  62.6 0.6 copy.10

commit v4 on v3

--- a/solution.py
+++ b/solution.py
@@ -13,6 +13,8 @@
 EXT = CZ + 2 * H
 FIRST, LAST, BELOW, ABOVE = H, H + CZ - 1, 0, H + CZ
 NX_CHIPS, NY, NZL = 4, 8, 6
+FARTHEST = [(dx, dz) for dz in range(2 * NZL) for dx in range(NX_CHIPS) if dx or dz]
+FARTHEST.sort(key=lambda d: -(min(d[0], NX_CHIPS - d[0]) + min(d[1], 2 * NZL - d[1])))
 PAIRS = [(0, 0), (0, 1), (0, 2), (0, 3), (1, 1), (1, 2), (1, 3), (2, 2), (2, 3)]
 
 
@@ -333,11 +335,9 @@
     send_row[...] = own_row
     ex[pl.ds(zl * N_IN + inn, 1), :] = own_row
     n_plane = 2 * NZL * NX_CHIPS
-    for dz in range(2 * NZL):
-        for dx in range(NX_CHIPS):
-            if dx or dz:
-                spot = ex.at[pl.ds(zl * N_IN + inn, 1)]
-                remote(send_row, spot, send_sem.at[8], recv_sem.at[8], plane_peer(dx, dz)).start()
+    spot = ex.at[pl.ds(zl * N_IN + inn, 1)]
+    for dx, dz in FARTHEST:
+        remote(send_row, spot, send_sem.at[8], recv_sem.at[8], plane_peer(dx, dz)).start()
     arrived = ex.at[pl.ds(0, n_plane - 1)]
     remote(arrived, arrived, send_sem.at[8], recv_sem.at[8], in_peer(1)).wait()
 
@@ -415,7 +415,7 @@
     spot_row = pl.multiple_of(y * 16 + core * 8, 8)
     ag[pl.ds(spot_row, 8), :] = units
     mine = ag.at[pl.ds(spot_row, 8)]
-    for k in range(NY):
+    for k in sorted(range(NY), key=lambda k: -min(k, NY - k)):
         for o in (0, 1):
             if k or o:
                 remote(mine, mine, send_sem.at[9], recv_sem.at[9], y_peer(k, o)).start()

time: 63.4 us -> 63.2 us (level)
  no operation moved by 1% of the time
where the time goes in v4:
time: 63.2 us; the launch traced here: 63 us
  Pallas kernels  61 us (97%)
  local copies, waits for them, and re-layouts  1.4 us (2%)
  between operations  0.64 us (1%)
    pallas_call x1, Pallas kernels, on_device(): pl.pallas_call(kernel, out_shape=(pltpu.VMEM((COMP, CZ, PY, PX), f32), pl...  61 us
    unnamed x2, local copies, waits for them, and re-layouts  1.4 us

profile of v4, /device:TPU:1, one launch (start us, length us, event | category | flops | bytes accessed | tf_op | source)
XLA Modules:
  0.0 63.0 jit_solution(17502145536633719832)
XLA Ops:
  0.6 61.0 %shard_map.68 = (f32[4,8,32,128]{3,2,1,0:T(8,128)S(1)}, f32[1,4,8,32]{3,2,1,0:T(8,128)S(1)}) custom-call(f32[4,8,32,128]{3,2,1,0:T(8,128)} %b_hbm.1, s32[8,32,128]{2,1,0:T(8,128)} %m_hbm.1, f32[4,4,8]{2,1,0:T(4,128)} %bitcast.2, s32[1,8]{1,0:T(1,128)} %bitcast.3, f32[8,6144]{1,0:T(8,128)} %cinv_hbm.1), custom_call_target="tpu_custom_call" | custom-call | tf_op jit(solution)/shard_map/pallas_call | solution.py:490
  61.6 0.8 %copy.9 = f32[4,8,32,128]{3,2,1,0:T(8,128)} copy(f32[4,8,32,128]{3,2,1,0:T(8,128)S(1)} %get-tuple-element.2) | data formatting | bytes 1048576
  62.4 0.6 copy.10
